TPU v7x, 32 devices: a whole 2x2x4 slice. The times are simulated.
32 devices in a mesh: circ: 8 (over z, y), side: 4 (over x, core).
Axes of the slice: x: 2, y: 2, z: 4, core: 2. Of those that a mesh axis runs over, the one named last changes fastest.
Arguments:
- field: float32 [4, 7, 7, 7, 8, 1024], P('side', None, None, None, None, 'circ'), may hold values from -6 to 6
- coeffs: float32 [4, 3, 7, 7, 7, 8, 1024], P('side', None, None, None, None, None, 'circ'), may hold values from 0.25 to 1.5
- reaction: float32 [4, 7, 7, 7, 8, 1024], P('side', None, None, None, None, 'circ'), may hold values from 0.25 to 8
- step_scale: float32 [4, 7, 7, 7, 8, 1024], P('side', None, None, None, None, 'circ'), may hold values from 0.0001 to 0.0003
- rotation: int32 [4], replicated, may hold values from 0 to 3071
Outputs:
- advanced: float32 [4, 7, 7, 7, 8, 1024], P('side', None, None, None, None, 'circ')
Inputs may be any that keep to these rules, and one draw needn't show every extreme that they name: `rotation`: rotor position in units of one 3-th of an element's circumferential width.
All inputs are finite; a program needn't handle non-finite values.
Results may differ from a plain program's by a relative error of at most 0.0001.
Values sent between devices are 32-bit elements; how exact they have to be, the bound alone decides.
A program may use at most 128 MiB of HBM per device.

v0:
```python
from functools import partial

import jax
import jax.numpy as jnp
import numpy as np
from jax import lax
from jax.experimental import pallas as pl
from jax.experimental.pallas import tpu as pltpu
from jax.sharding import PartitionSpec as P

SUBSTEPS = 3
STEPS = 4


def passed_along(value, axis, steps):
    count = lax.axis_size(axis)
    pairs = [(source, (source + steps) % count) for source in range(count)]
    return lax.ppermute(value, axis, pairs)


def padded_2(block, sides, width, periodic):
    for axis, dim in sides:
        count = lax.axis_size(axis)
        forward = [(i, i + 1) for i in range(count - 1)]
        if periodic:
            forward.append((count - 1, 0))
        backward = [(target, source) for source, target in forward]
        low = lax.ppermute(
            lax.slice_in_dim(block, block.shape[dim] - width, None, axis=dim), axis, forward
        )
        high = lax.ppermute(lax.slice_in_dim(block, 0, width, axis=dim), axis, backward)
        block = jnp.concatenate([low, block, high], axis=dim)
    return block


def gll_points():
    return np.array(
        [
            -1.0,
            -0.830223896278567,
            -0.4688487934707142,
            0.0,
            0.4688487934707142,
            0.830223896278567,
            1.0,
        ]
    )


def derivative_table():
    points = gll_points()
    node_count = points.shape[0]
    weights = np.array(
        [
            1.0 / np.prod([points[j] - points[k] for k in range(node_count) if k != j])
            for j in range(node_count)
        ]
    )
    derivative = np.zeros((node_count, node_count))
    for i in range(node_count):
        for j in range(node_count):
            if i != j:
                derivative[i, j] = weights[j] / weights[i] / (points[i] - points[j])
        derivative[i, i] = -np.sum(derivative[i])
    return derivative


def lagrange_rows(locations):
    points = gll_points()
    identity_mask = np.eye(7) > 0.5
    differences = np.array(
        [[1.0 if q == n else points[n] - points[q] for q in range(7)] for n in range(7)]
    )
    denominator = np.prod(differences, axis=1)
    distances = locations[:, None] - jnp.asarray(points, jnp.float32)[None, :]
    factors = jnp.where(identity_mask[None, :, :], 1.0, distances[:, None, :])
    return jnp.prod(factors, axis=2) / jnp.asarray(denominator, jnp.float32)[None, :]


def mortar_tables(fraction):
    heights = (1.0 + jnp.asarray(gll_points(), jnp.float32)) * 0.5
    on_right = heights >= fraction
    shifted_height = jnp.where(on_right, heights - fraction, heights - fraction + 1.0)
    values = lagrange_rows(2.0 * shifted_height - 1.0)
    from_right = jnp.where(on_right[:, None], values, 0.0)
    from_left = jnp.where(on_right[:, None], 0.0, values)
    return (from_left, from_right)


def element_apply(field, coeffs, reaction):
    derivative = jnp.asarray(derivative_table(), jnp.float32)
    highest = lax.Precision.HIGHEST
    grad_axial = jnp.einsum("pa,arcxe->prcxe", derivative, field, precision=highest)
    grad_radial = jnp.einsum("pr,arcxe->apcxe", derivative, field, precision=highest)
    grad_circ = jnp.einsum("pc,arcxe->arpxe", derivative, field, precision=highest)
    result = reaction * field
    result = result + jnp.einsum(
        "pa,prcxe->arcxe", derivative, coeffs[0] * grad_axial, precision=highest
    )
    result = result + jnp.einsum(
        "pr,apcxe->arcxe", derivative, coeffs[1] * grad_radial, precision=highest
    )
    result = result + jnp.einsum(
        "pc,arpxe->arcxe", derivative, coeffs[2] * grad_circ, precision=highest
    )
    return result


def fixed_pair(hops, circ_count, is_stator, data):
    ahead = passed_along(data, "circ", hops)
    behind = passed_along(data, "circ", (circ_count - hops - 1) % circ_count)
    return jnp.where(is_stator, ahead, behind)


def rotate_window(block, amount, whole_k, is_stator):
    edge_count = block.shape[-1]
    circ_count = lax.axis_size("circ")
    within = amount % edge_count
    sector_k = whole_k // edge_count
    branches = [partial(fixed_pair, hops, circ_count, is_stator) for hops in range(circ_count)]
    rotated = lax.switch(sector_k, branches, block)
    before = passed_along(rotated, "circ", 1)
    joined = jnp.concatenate([before, rotated], axis=3)
    first_index = edge_count - within - 1
    return lax.dynamic_slice_in_dim(joined, first_index, edge_count + 1, 3)


def project_mortar(incoming, amount, whole_k, is_stator, first_table, second_table):
    highest = lax.Precision.HIGHEST
    window = rotate_window(incoming, amount, whole_k, is_stator)
    edge_count = incoming.shape[-1]
    result = jnp.einsum(
        "mn,rnxe->rmxe", first_table, window[:, :, :, :edge_count], precision=highest
    )
    return result + jnp.einsum(
        "mn,rnxe->rmxe", second_table, window[:, :, :, 1:], precision=highest
    )


def local(field, coeffs, reaction, step_scale, rotation):
    side_index = lax.axis_index("side")
    lower = lax.axis_size("side") // 2 - 1
    cycle_length = field.shape[-1] * lax.axis_size("circ")
    is_stator = side_index > lower
    current = field[0]
    for step in range(STEPS):
        applied = element_apply(current, coeffs[0], reaction[0])
        zero_row = jnp.zeros_like(applied[:, 0, :, :1])
        summed = applied.at[:, 6].add(jnp.concatenate([applied[:, 0, :, 1:], zero_row], axis=2))
        summed = summed.at[:, 0].add(jnp.concatenate([zero_row, applied[:, 6, :, :-1]], axis=2))
        sector_rims = jnp.stack([applied[:, :, 0], applied[:, :, 6]])
        padded = padded_2(sector_rims, (("circ", 4),), 1, True)
        summed = summed.at[:, :, 6].add(padded[0, :, :, :, 2:])
        summed = summed.at[:, :, 0].add(padded[1, :, :, :, :-2])
        axial_faces = jnp.stack([applied[0], applied[6]])
        layered = padded_2(axial_faces, (("side", 0),), 1, False)
        below_top = layered[0]
        above_bottom = layered[3]
        offset = rotation[step]
        whole_k = offset // SUBSTEPS
        fraction = (offset % SUBSTEPS).astype(jnp.float32) / SUBSTEPS
        from_left, from_right = mortar_tables(fraction)
        first_table = jnp.where(is_stator, from_left, from_right.T)
        second_table = jnp.where(is_stator, from_right, from_left.T)
        amount = jnp.where(is_stator, whole_k, cycle_length - whole_k - 1)
        incoming = jnp.where(is_stator, below_top, above_bottom)
        contribution = project_mortar(
            incoming, amount, whole_k, is_stator, first_table, second_table
        )
        bottom_add = jnp.where(side_index == lower + 1, contribution, below_top)
        top_add = jnp.where(side_index == lower, contribution, above_bottom)
        summed = summed.at[0].add(bottom_add)
        summed = summed.at[6].add(top_add)
        current = current - step_scale[0] * summed
    return current[None]


N = 7
MESH = pl.DeviceIdType.MESH
CHUNKS = ((0, 4), (4, 3))


def half_tables(matrix):
    minus = 0.5 * (matrix[:3, :3] - matrix[:3, :3:-1])
    plus = 0.5 * (matrix[:3, :3] + matrix[:3, :3:-1])
    return minus, plus


def weighted(constants, values):
    total = float(constants[0]) * values[0]
    for constant, value in zip(constants[1:], values[1:]):
        total = total + float(constant) * value
    return total


def derivative_of(u):
    table = derivative_table()
    minus, plus = half_tables(table)
    odd = [u[j] - u[6 - j] for j in range(3)]
    twice = u[3] + u[3]
    even = [(u[j] + u[6 - j]) - twice for j in range(3)]
    p = [weighted(minus[i], odd) for i in range(3)]
    q = [weighted(plus[i], even) for i in range(3)]
    middle = weighted(table[3, :3], odd)
    return [p[i] + q[i] for i in range(3)] + [middle] + [p[i] - q[i] for i in (2, 1, 0)]


def transposed_of(w):
    table = derivative_table().T
    minus, plus = half_tables(table)
    odd = [w[j] - w[6 - j] for j in range(3)]
    even = [w[j] + w[6 - j] for j in range(3)] + [w[3]]
    p = [weighted(minus[i], odd) for i in range(3)]
    q = [weighted(list(plus[i]) + [table[i, 3]], even) for i in range(3)]
    middle = -2.0 * (p[0] + p[1] + p[2])
    return [p[i] + q[i] for i in range(3)] + [middle] + [p[i] - q[i] for i in (2, 1, 0)]


def mortar_constants():
    points = gll_points()
    heights = (1.0 + points) * 0.5
    tables = np.zeros((SUBSTEPS, N, N), np.float32)
    on_left = np.zeros((SUBSTEPS, N), np.int32)
    for f in range(SUBSTEPS):
        fraction = f / SUBSTEPS
        for m in range(N):
            left = heights[m] < fraction
            on_left[f, m] = left
            place = 2.0 * (heights[m] - fraction + left) - 1.0
            for n in range(N):
                others = [q for q in range(N) if q != n]
                tables[f, m, n] = np.prod(
                    [(place - points[q]) / (points[n] - points[q]) for q in others]
                )
    return tables.reshape(-1), on_left.reshape(-1)


def rotated(value, shift, lane, sectors):
    width = value.shape[1]
    within = lax.rem(shift, width)
    whole = lax.rem(lax.div(shift, width), sectors)
    turned = pltpu.roll(value, within, 1)
    near = pltpu.roll(turned, whole, 0)
    far = pltpu.roll(near, 1, 0)
    return jnp.where(lane >= within, near, far)


def paired(index, mask, count):
    result, bit = 0, 1
    while bit < count:
        flip = (mask // bit) % 2
        result = result + bit * lax.rem(lax.div(index, bit) + flip, 2)
        bit *= 2
    return result


def step_kernel(
    lower, circ_count, rot_ref, table_ref, left_ref, field_ref, coeffs_ref, reaction_ref,
    scale_ref, out_ref, U, K, R, S, A, G, O, M, C, B, ends, ends_in, load_sem, store_sem,
    conf_send, conf_recv, end_send, end_recv, one_send, one_recv, two_send, two_recv, own_sem,
):
    circ = lax.axis_index("circ")
    side = lax.axis_index("side")
    odd = lax.rem(side, 2)
    conf_a = 6 - 6 * odd
    mort_a = 6 * odd
    mate = side + 1 - 2 * odd
    across = 2 * lower + 1 - side
    at_interface = jnp.logical_or(side == lower, side == lower + 1)
    ahead = lax.rem(circ + 1, circ_count)
    behind = lax.rem(circ + circ_count - 1, circ_count)
    width = U.shape[-1]
    rows = U.shape[-2]
    lane = lax.broadcasted_iota(jnp.int32, (rows, width), 1)
    row = lax.broadcasted_iota(jnp.int32, (rows, width), 0)

    loads = [
        pltpu.make_async_copy(field_ref.at[0], U, load_sem.at[0]),
        pltpu.make_async_copy(reaction_ref.at[0], R, load_sem.at[1]),
        pltpu.make_async_copy(coeffs_ref.at[0, 2], K.at[2], load_sem.at[2]),
        pltpu.make_async_copy(coeffs_ref.at[0, 1], K.at[1], load_sem.at[3]),
        pltpu.make_async_copy(coeffs_ref.at[0, 0], K.at[0], load_sem.at[4]),
        pltpu.make_async_copy(scale_ref.at[0], S, load_sem.at[5]),
    ]
    for load in loads:
        load.start()

    barrier = pltpu.get_barrier_semaphore()
    pl.semaphore_signal(
        barrier, inc=1, device_id={"circ": circ, "side": mate}, device_id_type=MESH
    )

    @pl.when(at_interface)
    def _():
        for d in range(circ_count):
            other = lax.rem(circ + d, circ_count)
            pl.semaphore_signal(
                barrier, inc=1, device_id={"circ": other, "side": across}, device_id_type=MESH
            )
            if d > 0:
                pl.semaphore_signal(
                    barrier, inc=1, device_id={"circ": other, "side": side}, device_id_type=MESH
                )
        pl.semaphore_wait(barrier, 2 * circ_count)

    @pl.when(jnp.logical_not(at_interface))
    def _():
        for other in (ahead, behind):
            pl.semaphore_signal(
                barrier, inc=1, device_id={"circ": other, "side": side}, device_id_type=MESH
            )
        pl.semaphore_wait(barrier, 3)

    derivative = derivative_table()
    is_odd = odd == 1
    column = [
        jnp.where(is_odd, float(derivative[p, 6]), float(derivative[p, 0])) for p in range(N)
    ]
    square = [
        jnp.where(is_odd, float(derivative[p, 6] ** 2), float(derivative[p, 0] ** 2))
        for p in range(N)
    ]
    planes = [jnp.where(is_odd, 0, N)] + list(range(1, N - 1)) + [jnp.where(is_odd, N, 6)]

    def line(direction, i, j, start=None):
        def at(p):
            return ((p, i, j), (i, p, j), (i, j, p))[direction]

        def to(p):
            return (planes[p], i, j) if direction == 0 else at(p)

        u = [U[at(p)] for p in range(N)]
        g = derivative_of(u)
        w = [g[p] * K[(direction,) + at(p)] for p in range(N)]
        y = transposed_of(w)
        for p in range(N):
            base = A[to(p)] if start is None else start(at(p), u[p])
            A[to(p)] = base + y[p]

    def reacted(at, u):
        return R[at] * u

    def mortar_start(at, u):
        _, r, c = at
        return B[0, r, c] + B[1, r, c] * u

    def circ_lines():
        @pl.loop(0, N - 1)
        def _(q):
            for r in range(N):
                line(2, q + 1 - odd, r, reacted)

    def radial_lines():
        @pl.loop(0, N - 1)
        def _(q):
            for c in range(N):
                line(1, q + 1 - odd, c)

    def partial_axial():
        @pl.loop(0, N)
        def _(r):
            for c in range(N):
                u = [U[p, r, c] for p in range(N)]
                u[0] = jnp.where(is_odd, u[0], 0.0)
                u[6] = jnp.where(is_odd, 0.0, u[6])
                g = derivative_of(u)
                total = column[0] * (g[0] * K[0, 0, r, c])
                for p in range(1, N):
                    total = total + column[p] * (g[p] * K[0, p, r, c])
                B[0, r, c] = total

    for load in loads[:3]:
        load.wait()
    circ_lines()
    loads[3].wait()
    radial_lines()
    loads[4].wait()
    partial_axial()

    @pl.loop(0, N)
    def _(r):
        for c in range(N):
            total = R[mort_a, r, c]
            for p in range(N):
                total = total + square[p] * K[0, p, r, c]
            B[1, r, c] = total

    loads[5].wait()

    def update_plane(a, from_ahead, from_behind, extra):
        for r in range(N):
            i = a * N + r
            for c in range(N):
                s = A[a, r, c]
                if r == 6:
                    s = s + jnp.where(row < rows - 1, pltpu.roll(A[a, 0, c], rows - 1, 0), 0.0)
                if r == 0:
                    s = s + jnp.where(row > 0, pltpu.roll(A[a, 6, c], 1, 0), 0.0)
                if c == 6:
                    s = s + jnp.where(
                        lane == width - 1,
                        pltpu.roll(from_ahead, width - 1 - i, 1),
                        pltpu.roll(A[a, r, 0], width - 1, 1),
                    )
                if c == 0:
                    s = s + jnp.where(
                        lane == 0,
                        pltpu.roll(from_behind, lax.rem(width - i, width), 1),
                        pltpu.roll(A[a, r, 6], 1, 1),
                    )
                if extra is not None:
                    s = s + extra[r, c]
                U[a, r, c] = U[a, r, c] - S[a, r, c] * s

    def one_step(t, _):
        par = lax.rem(t, 2)

        def conf_copy():
            return pltpu.make_async_remote_copy(
                src_ref=A.at[conf_a], dst_ref=C.at[par], send_sem=conf_send,
                recv_sem=conf_recv.at[par], device_id={"circ": circ, "side": mate},
                device_id_type=MESH,
            )

        def end_copy(which, target):
            return pltpu.make_async_remote_copy(
                src_ref=ends.at[which], dst_ref=ends_in.at[par, which],
                send_sem=end_send.at[which], recv_sem=end_recv.at[par, which],
                device_id={"circ": target, "side": side}, device_id_type=MESH,
            )

        def one_copy(h, d):
            rows_of = pl.ds(*CHUNKS[h])
            target = paired(circ, d, circ_count)
            return pltpu.make_async_remote_copy(
                src_ref=A.at[mort_a, rows_of, :, pl.ds(target, 1), :],
                dst_ref=G.at[par, rows_of, :, pl.ds(circ, 1), :],
                send_sem=one_send.at[h, d], recv_sem=one_recv.at[par, h, d],
                device_id={"circ": target, "side": across}, device_id_type=MESH,
            )

        def two_copy(h, d):
            rows_of = pl.ds(*CHUNKS[h])
            target = paired(circ, d, circ_count)
            return pltpu.make_async_remote_copy(
                src_ref=O.at[rows_of, :, pl.ds(target, 1), :],
                dst_ref=M.at[par, rows_of, :, pl.ds(circ, 1), :],
                send_sem=two_send.at[h, d], recv_sem=two_recv.at[par, h, d],
                device_id={"circ": target, "side": side}, device_id_type=MESH,
            )

        def own_copy():
            return pltpu.make_async_copy(
                O.at[:, :, pl.ds(circ, 1), :], M.at[par, :, :, pl.ds(circ, 1), :], own_sem
            )

        for q in range(N):
            line(2, mort_a, q, mortar_start)
        for q in range(N):
            line(1, mort_a, q)

        @pl.when(at_interface)
        def _():
            for h in range(len(CHUNKS)):
                for d in reversed(range(circ_count)):
                    one_copy(h, d).start()

        @pl.loop(0, N)
        def _(r):
            for c in range(N):
                line(0, r, c)

        conf_copy().start()

        def pack(a, carry):
            low, high = carry
            for r in range(N):
                i = a * N + r
                low = jnp.where(lane == i, pltpu.roll(A[a, r, 0], i, 1), low)
                high = jnp.where(lane == i, pltpu.roll(A[a, r, 6], i + 1, 1), high)
            return low, high

        zero = jnp.zeros((rows, width), jnp.float32)
        low, high = lax.fori_loop(0, N, pack, (zero, zero))
        ends[0] = low
        ends[1] = high
        end_copy(0, behind).start()
        end_copy(1, ahead).start()

        offset = rot_ref[t]
        k = lax.div(offset, SUBSTEPS)
        f = offset - SUBSTEPS * k
        cycle = circ_count * width

        def stator_rows(r):
            values = [G[par, r, n] for n in range(N)]
            for m in range(N):
                total = table_ref[f * N * N + m * N] * values[0]
                for n in range(1, N):
                    total = total + table_ref[f * N * N + m * N + n] * values[n]
                O[r, m] = rotated(total, k + left_ref[f * N + m], lane, circ_count)

        def rotor_rows(r):
            values = [
                rotated(G[par, r, m], cycle - k - left_ref[f * N + m], lane, circ_count)
                for m in range(N)
            ]
            for n in range(N):
                total = table_ref[f * N * N + n] * values[0]
                for m in range(1, N):
                    total = total + table_ref[f * N * N + m * N + n] * values[m]
                O[r, n] = total

        for h, (begin, count) in enumerate(CHUNKS):
            @pl.when(at_interface)
            def _():
                for d in range(circ_count):
                    one_copy(h, d).wait_recv()

            @pl.when(side == lower + 1)
            def _():
                pl.loop(begin, begin + count)(stator_rows)

            @pl.when(side == lower)
            def _():
                pl.loop(begin, begin + count)(rotor_rows)

            @pl.when(at_interface)
            def _():
                for d in reversed(range(1, circ_count)):
                    two_copy(h, d).start()

        @pl.when(at_interface)
        def _():
            own_copy().start()

        end_copy(0, behind).wait_recv()
        end_copy(1, ahead).wait_recv()
        from_ahead = ends_in[par, 0]
        from_behind = ends_in[par, 1]

        @pl.loop(1, N - 1)
        def _(a):
            update_plane(a, from_ahead, from_behind, None)

        conf_copy().wait_recv()
        update_plane(conf_a, from_ahead, from_behind, C.at[par])

        conf_copy().wait_send()

        @pl.when(t < STEPS - 1)
        def _():
            circ_lines()
            radial_lines()
            partial_axial()

        @pl.when(t == STEPS - 1)
        def _():
            early_store().start()

        @pl.when(at_interface)
        def _():
            own_copy().wait()
            for h in range(len(CHUNKS)):
                for d in range(1, circ_count):
                    two_copy(h, d).wait_recv()
            update_plane(mort_a, from_ahead, from_behind, M.at[par])
            for h in range(len(CHUNKS)):
                for d in range(circ_count):
                    one_copy(h, d).wait_send()
                for d in range(1, circ_count):
                    two_copy(h, d).wait_send()

        @pl.when(jnp.logical_not(at_interface))
        def _():
            update_plane(mort_a, from_ahead, from_behind, None)

        end_copy(0, behind).wait_send()
        end_copy(1, ahead).wait_send()
        return 0

    def early_store():
        others = pl.ds(1 - odd, N - 1)
        return pltpu.make_async_copy(U.at[others], out_ref.at[0, others], store_sem.at[0])

    lax.fori_loop(0, STEPS, one_step, 0)
    late = pltpu.make_async_copy(U.at[mort_a], out_ref.at[0, mort_a], store_sem.at[1])
    late.start()
    early_store().wait()
    late.wait()


def fused(mesh, field, coeffs, reaction, step_scale, rotation):
    circ_count = mesh.shape["circ"]
    lower = mesh.shape["side"] // 2 - 1
    node_shape = field.shape[1:]
    face_shape = node_shape[1:]
    tile = face_shape[2:]
    tables, on_left = mortar_constants()
    smem = pl.BlockSpec(memory_space=pltpu.SMEM)
    anywhere = pl.BlockSpec(memory_space=pl.ANY)
    dma = pltpu.SemaphoreType.DMA
    f32 = jnp.float32
    return pl.pallas_call(
        partial(step_kernel, lower, circ_count),
        out_shape=jax.ShapeDtypeStruct(field.shape, f32),
        in_specs=[smem, smem, smem] + [anywhere] * 4,
        out_specs=anywhere,
        scratch_shapes=[
            pltpu.VMEM(node_shape, f32),
            pltpu.VMEM(coeffs.shape[1:], f32),
            pltpu.VMEM(node_shape, f32),
            pltpu.VMEM(node_shape, f32),
            pltpu.VMEM((N + 1,) + face_shape, f32),
            pltpu.VMEM((2,) + face_shape, f32),
            pltpu.VMEM(face_shape, f32),
            pltpu.VMEM((2,) + face_shape, f32),
            pltpu.VMEM((2,) + face_shape, f32),
            pltpu.VMEM((2,) + face_shape, f32),
            pltpu.VMEM((2,) + tile, f32),
            pltpu.VMEM((2, 2) + tile, f32),
            dma((6,)),
            dma((2,)),
            dma(()),
            dma((2,)),
            dma((2,)),
            dma((2, 2)),
            dma((len(CHUNKS), circ_count)),
            dma((2, len(CHUNKS), circ_count)),
            dma((len(CHUNKS), circ_count)),
            dma((2, len(CHUNKS), circ_count)),
            dma(()),
        ],
        compiler_params=pltpu.CompilerParams(collective_id=0, has_side_effects=True),
    )(rotation, jnp.asarray(tables), jnp.asarray(on_left), field, coeffs, reaction, step_scale)


def solution(mesh):
    def body(field, coeffs, reaction, step_scale, rotation):
        radial_count, lanes = field.shape[-2:]
        whole_circle = radial_count == mesh.shape["circ"] == 8 and lanes == 128
        if whole_circle and mesh.shape["side"] == 4:
            return fused(mesh, field, coeffs, reaction, step_scale, rotation)
        return local(field, coeffs, reaction, step_scale, rotation)

    in_specs = (
        P("side", None, None, None, None, "circ"),
        P("side", None, None, None, None, None, "circ"),
        P("side", None, None, None, None, "circ"),
        P("side", None, None, None, None, "circ"),
        P(),
    )
    out_specs = P("side", None, None, None, None, "circ")
    return jax.shard_map(body, mesh=mesh, in_specs=in_specs, out_specs=out_specs, check_vma=False)
```

profile of v0, /device:TPU:1, one launch (start us, length us, event | category | flops | bytes accessed | tf_op | source)
XLA Modules:
  0.0 53.5 jit_solution(7270213851442034337)
XLA Ops:
  0.0 51.0 %shard_map.73 = f32[1,7,7,7,8,128]{5,4,3,2,1,0:T(8,128)} custom-call(s32[4]{0:T(128)} %rot_ref.1, f32[147]{0:T(256)} %constant.4.clone.table_ref, s32[21]{0:T(128)} %constant.5.clone.left_ref, f32[1,7,7,7,8,128]{5,4,3,2,1,0:T(8,128)} %field_ref.1, f32[1,3,7,7,7,8,128]{6,5,4,3,2,1,0:T(8,128)} %coeffs_ref.1, f32[1,7,7,7,8,128]{5,4,3,2,1,0:T(8,128)} %reaction_ref.1, ...), custom_call_target="tpu_custom_call" | custom-call | tf_op jit(solution)/shard_map/pallas_call | solution.py:604
  51.0 2.5 %copy.9 = f32[1,7,7,7,8,128]{5,4,3,2,1,0:T(8,128)} copy(f32[1,7,7,7,8,128]{5,4,3,2,1,0:T(8,128)} %shard_map.73) | data formatting | bytes 2809856
where the time goes:
time: 53.7 us; the launch traced here: 53.5 us
  Pallas kernels  51 us (95%)
  local copies, waits for them, and re-layouts  2.53 us (5%)
    pallas_call x1, Pallas kernels, fused(): pl.pallas_call(partial(step_kernel, lower, circ_count), out_shape=jax.Sha...  51 us
    unnamed x1, local copies, waits for them, and re-layouts  2.53 us

commit v1 on v0

--- a/solution.py
+++ b/solution.py
@@ -177,7 +177,7 @@
 
 N = 7
 MESH = pl.DeviceIdType.MESH
-CHUNKS = ((0, 4), (4, 3))
+CHUNKS = ((0, 3), (3, 2), (5, 2))
 
 
 def half_tables(matrix):
@@ -301,7 +301,6 @@
                 pl.semaphore_signal(
                     barrier, inc=1, device_id={"circ": other, "side": side}, device_id_type=MESH
                 )
-        pl.semaphore_wait(barrier, 2 * circ_count)
 
     @pl.when(jnp.logical_not(at_interface))
     def _():
@@ -309,7 +308,15 @@
             pl.semaphore_signal(
                 barrier, inc=1, device_id={"circ": other, "side": side}, device_id_type=MESH
             )
-        pl.semaphore_wait(barrier, 3)
+
+    def barrier_wait():
+        @pl.when(at_interface)
+        def _():
+            pl.semaphore_wait(barrier, 2 * circ_count)
+
+        @pl.when(jnp.logical_not(at_interface))
+        def _():
+            pl.semaphore_wait(barrier, 3)
 
     derivative = derivative_table()
     is_odd = odd == 1
@@ -386,6 +393,7 @@
             B[1, r, c] = total
 
     loads[5].wait()
+    barrier_wait()
 
     def update_plane(a, from_ahead, from_behind, extra):
         for r in range(N):

time: 53.7 us -> 51.2 us (0.953)
  Pallas kernels: 51 us -> 48.5 us
    pallas_call x1, Pallas kernels: 51 us -> 48.5 us  [fused(): pl.pallas_call(partial(step_kernel, lower, circ_count), out_shape=jax.Sha...]
where the time goes in v1:
time: 51.2 us; the launch traced here: 51.1 us
  Pallas kernels  48.5 us (95%)
  local copies, waits for them, and re-layouts  2.53 us (5%)
    pallas_call x1, Pallas kernels, fused(): pl.pallas_call(partial(step_kernel, lower, circ_count), out_shape=jax.Sha...  48.5 us
    unnamed x1, local copies, waits for them, and re-layouts  2.53 us

profile of v1, /device:TPU:1, one launch (start us, length us, event | category | flops | bytes accessed | tf_op | source)
XLA Modules:
  0.0 51.1 jit_solution(13088018491307577382)
XLA Ops:
  0.0 48.5 %shard_map.73 = f32[1,7,7,7,8,128]{5,4,3,2,1,0:T(8,128)} custom-call(s32[4]{0:T(128)} %rot_ref.1, f32[147]{0:T(256)} %constant.4.clone.table_ref, s32[21]{0:T(128)} %constant.5.clone.left_ref, f32[1,7,7,7,8,128]{5,4,3,2,1,0:T(8,128)} %field_ref.1, f32[1,3,7,7,7,8,128]{6,5,4,3,2,1,0:T(8,128)} %coeffs_ref.1, f32[1,7,7,7,8,128]{5,4,3,2,1,0:T(8,128)} %reaction_ref.1, ...), custom_call_target="tpu_custom_call" | custom-call | tf_op jit(solution)/shard_map/pallas_call | solution.py:612
  48.6 2.5 %copy.9 = f32[1,7,7,7,8,128]{5,4,3,2,1,0:T(8,128)} copy(f32[1,7,7,7,8,128]{5,4,3,2,1,0:T(8,128)} %shard_map.73) | data formatting | bytes 2809856

commit v2 on v0

--- a/solution.py
+++ b/solution.py
@@ -177,7 +177,10 @@
 
 N = 7
 MESH = pl.DeviceIdType.MESH
-CHUNKS = ((0, 4), (4, 3))
+CHUNKS = ((0, 3), (3, 4))
+RIMS = (0, 6)
+INNER = (1, 2, 3, 4, 5)
+FAR_FIRST = (5, 4, 7, 6, 3, 2, 1, 0)
 
 
 def half_tables(matrix):
@@ -255,18 +258,32 @@
 
 
 def step_kernel(
-    lower, circ_count, rot_ref, table_ref, left_ref, field_ref, coeffs_ref, reaction_ref,
-    scale_ref, out_ref, U, K, R, S, A, G, O, M, C, B, ends, ends_in, load_sem, store_sem,
-    conf_send, conf_recv, end_send, end_recv, one_send, one_recv, two_send, two_recv, own_sem,
+    lower, circ_count, first, workers, work_sides, rot_ref, table_ref, left_ref, field_ref,
+    coeffs_ref, reaction_ref, scale_ref, out_ref, K, R, S, A, G, O, M, C, B, ends, ends_in,
+    load_sem, conf_send, conf_recv, end_send, end_recv, one_send, one_recv, two_send, two_recv,
 ):
+    U = out_ref.at[0]
     circ = lax.axis_index("circ")
     side = lax.axis_index("side")
     odd = lax.rem(side, 2)
     conf_a = 6 - 6 * odd
     mort_a = 6 * odd
     mate = side + 1 - 2 * odd
-    across = 2 * lower + 1 - side
     at_interface = jnp.logical_or(side == lower, side == lower + 1)
+    own_way = jnp.where(side == lower, 0, 1)
+    central = jnp.logical_and(circ >= first, circ < first + workers)
+    is_worker, side_place = [], []
+    for sides in work_sides:
+        is_here = side == sides[0]
+        place = 0
+        for i in range(1, len(sides)):
+            is_here = jnp.logical_or(is_here, side == sides[i])
+            place = place + jnp.where(side == sides[i], i, 0)
+        is_worker.append(jnp.logical_and(central, is_here))
+        side_place.append(place)
+    slots = G.shape[1]
+    locals_count = G.shape[2]
+    near = 2 * lax.div(circ, circ_count // 2) + lax.rem(circ, 2)
     ahead = lax.rem(circ + 1, circ_count)
     behind = lax.rem(circ + circ_count - 1, circ_count)
     width = U.shape[-1]
@@ -274,15 +291,21 @@
     lane = lax.broadcasted_iota(jnp.int32, (rows, width), 1)
     row = lax.broadcasted_iota(jnp.int32, (rows, width), 0)
 
-    loads = [
+    others = pl.ds(1 - odd, N - 1)
+    face_loads = [
         pltpu.make_async_copy(field_ref.at[0], U, load_sem.at[0]),
-        pltpu.make_async_copy(reaction_ref.at[0], R, load_sem.at[1]),
-        pltpu.make_async_copy(coeffs_ref.at[0, 2], K.at[2], load_sem.at[2]),
-        pltpu.make_async_copy(coeffs_ref.at[0, 1], K.at[1], load_sem.at[3]),
-        pltpu.make_async_copy(coeffs_ref.at[0, 0], K.at[0], load_sem.at[4]),
-        pltpu.make_async_copy(scale_ref.at[0], S, load_sem.at[5]),
+        pltpu.make_async_copy(coeffs_ref.at[0, 0], K.at[0], load_sem.at[1]),
+        pltpu.make_async_copy(reaction_ref.at[0, mort_a], R.at[mort_a], load_sem.at[2]),
+        pltpu.make_async_copy(coeffs_ref.at[0, 1, mort_a], K.at[1, mort_a], load_sem.at[3]),
+        pltpu.make_async_copy(coeffs_ref.at[0, 2, mort_a], K.at[2, mort_a], load_sem.at[4]),
     ]
-    for load in loads:
+    later_loads = [
+        pltpu.make_async_copy(reaction_ref.at[0, others], R.at[others], load_sem.at[5]),
+        pltpu.make_async_copy(coeffs_ref.at[0, 1, others], K.at[1, others], load_sem.at[6]),
+        pltpu.make_async_copy(coeffs_ref.at[0, 2, others], K.at[2, others], load_sem.at[7]),
+        pltpu.make_async_copy(scale_ref.at[0], S, load_sem.at[8]),
+    ]
+    for load in face_loads + later_loads:
         load.start()
 
     barrier = pltpu.get_barrier_semaphore()
@@ -290,26 +313,34 @@
         barrier, inc=1, device_id={"circ": circ, "side": mate}, device_id_type=MESH
     )
 
-    @pl.when(at_interface)
-    def _():
-        for d in range(circ_count):
-            other = lax.rem(circ + d, circ_count)
+    def greet(other_circ, other_side, when):
+        same = jnp.logical_and(circ == other_circ, side == other_side)
+
+        @pl.when(jnp.logical_and(when, jnp.logical_not(same)))
+        def _():
             pl.semaphore_signal(
-                barrier, inc=1, device_id={"circ": other, "side": across}, device_id_type=MESH
+                barrier, inc=1, device_id={"circ": other_circ, "side": other_side},
+                device_id_type=MESH,
             )
-            if d > 0:
-                pl.semaphore_signal(
-                    barrier, inc=1, device_id={"circ": other, "side": side}, device_id_type=MESH
-                )
-        pl.semaphore_wait(barrier, 2 * circ_count)
-
-    @pl.when(jnp.logical_not(at_interface))
-    def _():
-        for other in (ahead, behind):
-            pl.semaphore_signal(
-                barrier, inc=1, device_id={"circ": other, "side": side}, device_id_type=MESH
-            )
-        pl.semaphore_wait(barrier, 3)
+
+    greeted = 3
+    for other in (ahead, behind):
+        pl.semaphore_signal(
+            barrier, inc=1, device_id={"circ": other, "side": side}, device_id_type=MESH
+        )
+    for way, sides in enumerate(work_sides):
+        meets_self = jnp.logical_and(at_interface, is_worker[way]).astype(jnp.int32)
+        for work_side in sides:
+            for w in range(first, first + workers):
+                greet(w, work_side, at_interface)
+        for c in range(circ_count):
+            for face_side in (lower, lower + 1):
+                greet(c, face_side, is_worker[way])
+        greeted = greeted + jnp.where(at_interface, workers * len(sides), 0) - meets_self
+        greeted = greeted + jnp.where(is_worker[way], 2 * circ_count, 0) - meets_self
+
+    def barrier_wait():
+        pl.semaphore_wait(barrier, greeted)
 
     derivative = derivative_table()
     is_odd = odd == 1
@@ -344,22 +375,18 @@
         _, r, c = at
         return B[0, r, c] + B[1, r, c] * u
 
-    def circ_lines():
-        @pl.loop(0, N - 1)
-        def _(q):
-            for r in range(N):
-                line(2, q + 1 - odd, r, reacted)
-
-    def radial_lines():
-        @pl.loop(0, N - 1)
-        def _(q):
-            for c in range(N):
-                line(1, q + 1 - odd, c)
-
-    def partial_axial():
+    def circ_lines(plane):
+        for r in range(N):
+            line(2, plane, r)
+
+    def radial_lines(plane, columns):
+        for c in columns:
+            line(1, plane, c, reacted)
+
+    def partial_axial(columns):
         @pl.loop(0, N)
         def _(r):
-            for c in range(N):
+            for c in columns:
                 u = [U[p, r, c] for p in range(N)]
                 u[0] = jnp.where(is_odd, u[0], 0.0)
                 u[6] = jnp.where(is_odd, 0.0, u[6])
@@ -369,13 +396,25 @@
                     total = total + column[p] * (g[p] * K[0, p, r, c])
                 B[0, r, c] = total
 
-    for load in loads[:3]:
+    def first_lines():
+        for load in later_loads[:2]:
+            load.wait()
+
+        @pl.loop(0, N - 1)
+        def _(q):
+            radial_lines(q + 1 - odd, range(N))
+
+        later_loads[2].wait()
+
+        @pl.loop(0, N - 1)
+        def _(q):
+            circ_lines(q + 1 - odd)
+
+        later_loads[3].wait()
+
+    for load in face_loads:
         load.wait()
-    circ_lines()
-    loads[3].wait()
-    radial_lines()
-    loads[4].wait()
-    partial_axial()
+    partial_axial(range(N))
 
     @pl.loop(0, N)
     def _(r):
@@ -385,12 +424,12 @@
                 total = total + square[p] * K[0, p, r, c]
             B[1, r, c] = total
 
-    loads[5].wait()
-
-    def update_plane(a, from_ahead, from_behind, extra):
+    barrier_wait()
+
+    def update_plane(a, columns, from_ahead, from_behind, extra):
         for r in range(N):
             i = a * N + r
-            for c in range(N):
+            for c in columns:
                 s = A[a, r, c]
                 if r == 6:
                     s = s + jnp.where(row < rows - 1, pltpu.roll(A[a, 0, c], rows - 1, 0), 0.0)
@@ -429,170 +468,227 @@
                 device_id={"circ": target, "side": side}, device_id_type=MESH,
             )
 
-        def one_copy(h, d):
+        def remote(src, dst, send_sem, recv_sem, to_circ, to_side):
+            return pltpu.make_async_remote_copy(
+                src_ref=src, dst_ref=dst, send_sem=send_sem, recv_sem=recv_sem,
+                device_id={"circ": to_circ, "side": to_side}, device_id_type=MESH,
+            )
+
+        def start(src, dst, send_sem, recv_sem, to_circ, to_side, can_be_here):
+            copy = remote(src, dst, send_sem, recv_sem, to_circ, to_side)
+            if not can_be_here:
+                copy.start()
+                return
+            here = jnp.logical_and(to_circ == circ, to_side == side)
+
+            @pl.when(jnp.logical_not(here))
+            def _():
+                copy.start()
+
+            @pl.when(here)
+            def _():
+                pltpu.make_async_copy(src, dst, recv_sem).start()
+
+        def wait_sent(sent, send_sem, one_here):
+            def wait(ref):
+                remote(ref, ref, send_sem, send_sem, circ, mate).wait_send()
+
+            @pl.when(one_here)
+            def _():
+                wait(sent.at[..., pl.ds(0, rows - 1), :])
+
+            @pl.when(jnp.logical_not(one_here))
+            def _():
+                wait(sent)
+
+        def arrived(ref, recv_sem):
+            remote(ref, ref, recv_sem, recv_sem, circ, mate).wait_recv()
+
+        own_slot = own_way if slots > 1 else 0
+
+        def start_one(h, d):
+            rows_of = pl.ds(*CHUNKS[h])
+            place = paired(near, d % workers, workers)
+            group = d // workers
+            at = group % len(work_sides[0])
+            start(
+                A.at[mort_a, rows_of, :, pl.ds(group * workers + place, 1), :],
+                G.at[par, own_slot, group // len(work_sides[0]), rows_of, :, pl.ds(circ, 1), :],
+                one_send, one_recv.at[par, h, own_slot], first + place,
+                jnp.where(side == lower, work_sides[0][at], work_sides[1][at]),
+                d % workers == 0 and any(lower + w == work_sides[w][at] for w in range(2)),
+            )
+
+        def start_two(way, h, j, d):
             rows_of = pl.ds(*CHUNKS[h])
             target = paired(circ, d, circ_count)
-            return pltpu.make_async_remote_copy(
-                src_ref=A.at[mort_a, rows_of, :, pl.ds(target, 1), :],
-                dst_ref=G.at[par, rows_of, :, pl.ds(circ, 1), :],
-                send_sem=one_send.at[h, d], recv_sem=one_recv.at[par, h, d],
-                device_id={"circ": target, "side": across}, device_id_type=MESH,
+            slot = way if slots > 1 else 0
+            place = (j * len(work_sides[way]) + side_place[way]) * workers + circ - first
+            start(
+                O.at[slot, j, rows_of, :, pl.ds(target, 1), :],
+                M.at[par, rows_of, :, pl.ds(place, 1), :],
+                two_send.at[slot], two_recv.at[par, h], target, lower + 1 - way,
+                d == 0 and lower + 1 - way in work_sides[way],
             )
 
-        def two_copy(h, d):
-            rows_of = pl.ds(*CHUNKS[h])
-            target = paired(circ, d, circ_count)
-            return pltpu.make_async_remote_copy(
-                src_ref=O.at[rows_of, :, pl.ds(target, 1), :],
-                dst_ref=M.at[par, rows_of, :, pl.ds(circ, 1), :],
-                send_sem=two_send.at[h, d], recv_sem=two_recv.at[par, h, d],
-                device_id={"circ": target, "side": side}, device_id_type=MESH,
-            )
-
-        def own_copy():
-            return pltpu.make_async_copy(
-                O.at[:, :, pl.ds(circ, 1), :], M.at[par, :, :, pl.ds(circ, 1), :], own_sem
-            )
-
         for q in range(N):
-            line(2, mort_a, q, mortar_start)
-        for q in range(N):
-            line(1, mort_a, q)
-
-        @pl.when(at_interface)
+            line(1, mort_a, q, mortar_start)
+        for h, (begin, count) in enumerate(CHUNKS):
+            for q in range(begin, begin + count):
+                line(2, mort_a, q)
+
+            @pl.when(at_interface)
+            def _():
+                for d in reversed(range(circ_count)):
+                    start_one(h, d)
+
+        @pl.when(t == 0)
         def _():
-            for h in range(len(CHUNKS)):
-                for d in reversed(range(circ_count)):
-                    one_copy(h, d).start()
-
-        @pl.loop(0, N)
-        def _(r):
-            for c in range(N):
-                line(0, r, c)
-
-        conf_copy().start()
-
-        def pack(a, carry):
-            low, high = carry
-            for r in range(N):
-                i = a * N + r
-                low = jnp.where(lane == i, pltpu.roll(A[a, r, 0], i, 1), low)
-                high = jnp.where(lane == i, pltpu.roll(A[a, r, 6], i + 1, 1), high)
-            return low, high
-
-        zero = jnp.zeros((rows, width), jnp.float32)
-        low, high = lax.fori_loop(0, N, pack, (zero, zero))
+            first_lines()
+
+        def axial_lines(columns):
+            @pl.loop(0, N)
+            def _(r):
+                for c in columns:
+                    line(0, r, c)
+
+        axial_lines(RIMS)
+        low = jnp.zeros((rows, width), jnp.float32)
+        high = low
+        for i in range(N * N):
+            low = jnp.where(lane == i, pltpu.roll(A[i // N, i % N, 0], i, 1), low)
+            high = jnp.where(lane == i, pltpu.roll(A[i // N, i % N, 6], i + 1, 1), high)
         ends[0] = low
         ends[1] = high
         end_copy(0, behind).start()
         end_copy(1, ahead).start()
+        axial_lines(INNER)
+        conf_copy().start()
+
+        def inner_plane(a, extra):
+            update_plane(a, INNER, None, None, extra)
+
+            @pl.when(t < STEPS - 1)
+            def _():
+                radial_lines(a, INNER)
+
+        @pl.loop(1, N - 1)
+        def _(a):
+            inner_plane(a, None)
+
+        conf_copy().wait_recv()
+        conf_copy().wait_send()
+        inner_plane(conf_a, C.at[par])
+
+        @pl.when(t < STEPS - 1)
+        def _():
+            partial_axial(INNER)
 
         offset = rot_ref[t]
         k = lax.div(offset, SUBSTEPS)
         f = offset - SUBSTEPS * k
         cycle = circ_count * width
 
-        def stator_rows(r):
-            values = [G[par, r, n] for n in range(N)]
+        def stator_rows(slot, places):
+            values = [[G[par, slot, j, r, n] for n in range(N)] for j, r in places]
             for m in range(N):
-                total = table_ref[f * N * N + m * N] * values[0]
-                for n in range(1, N):
-                    total = total + table_ref[f * N * N + m * N + n] * values[n]
-                O[r, m] = rotated(total, k + left_ref[f * N + m], lane, circ_count)
-
-        def rotor_rows(r):
+                factors = [table_ref[f * N * N + m * N + n] for n in range(N)]
+                shift = k + left_ref[f * N + m]
+                for (j, r), own in zip(places, values):
+                    total = factors[0] * own[0]
+                    for n in range(1, N):
+                        total = total + factors[n] * own[n]
+                    O[slot, j, r, m] = rotated(total, shift, lane, circ_count)
+
+        def rotor_rows(slot, places):
+            shifts = [cycle - k - left_ref[f * N + m] for m in range(N)]
             values = [
-                rotated(G[par, r, m], cycle - k - left_ref[f * N + m], lane, circ_count)
-                for m in range(N)
+                [rotated(G[par, slot, j, r, m], shifts[m], lane, circ_count) for m in range(N)]
+                for j, r in places
             ]
             for n in range(N):
-                total = table_ref[f * N * N + n] * values[0]
-                for m in range(1, N):
-                    total = total + table_ref[f * N * N + m * N + n] * values[m]
-                O[r, n] = total
+                factors = [table_ref[f * N * N + m * N + n] for m in range(N)]
+                for (j, r), own in zip(places, values):
+                    total = factors[0] * own[0]
+                    for m in range(1, N):
+                        total = total + factors[m] * own[m]
+                    O[slot, j, r, n] = total
 
         for h, (begin, count) in enumerate(CHUNKS):
-            @pl.when(at_interface)
-            def _():
-                for d in range(circ_count):
-                    one_copy(h, d).wait_recv()
-
-            @pl.when(side == lower + 1)
-            def _():
-                pl.loop(begin, begin + count)(stator_rows)
-
-            @pl.when(side == lower)
-            def _():
-                pl.loop(begin, begin + count)(rotor_rows)
-
-            @pl.when(at_interface)
-            def _():
-                for d in reversed(range(1, circ_count)):
-                    two_copy(h, d).start()
-
-        @pl.when(at_interface)
-        def _():
-            own_copy().start()
+            for way, project in enumerate((stator_rows, rotor_rows)):
+                @pl.when(is_worker[way])
+                def _():
+                    slot = way if slots > 1 else 0
+                    arrived(G.at[par, slot, :, pl.ds(begin, count)], one_recv.at[par, h, slot])
+                    for j in range(locals_count):
+                        project(slot, [(j, r) for r in range(begin, begin + count)])
+                        for d in FAR_FIRST:
+                            start_two(way, h, j, d)
 
         end_copy(0, behind).wait_recv()
         end_copy(1, ahead).wait_recv()
         from_ahead = ends_in[par, 0]
         from_behind = ends_in[par, 1]
 
+        def rim_plane(a, extra):
+            update_plane(a, RIMS, from_ahead, from_behind, extra)
+
+            @pl.when(t < STEPS - 1)
+            def _():
+                radial_lines(a, RIMS)
+                circ_lines(a)
+
         @pl.loop(1, N - 1)
         def _(a):
-            update_plane(a, from_ahead, from_behind, None)
-
-        conf_copy().wait_recv()
-        update_plane(conf_a, from_ahead, from_behind, C.at[par])
-
-        conf_copy().wait_send()
+            rim_plane(a, None)
+
+        rim_plane(conf_a, C.at[par])
 
         @pl.when(t < STEPS - 1)
         def _():
-            circ_lines()
-            radial_lines()
-            partial_axial()
-
-        @pl.when(t == STEPS - 1)
-        def _():
-            early_store().start()
+            partial_axial(RIMS)
 
         @pl.when(at_interface)
         def _():
-            own_copy().wait()
             for h in range(len(CHUNKS)):
-                for d in range(1, circ_count):
-                    two_copy(h, d).wait_recv()
-            update_plane(mort_a, from_ahead, from_behind, M.at[par])
-            for h in range(len(CHUNKS)):
-                for d in range(circ_count):
-                    one_copy(h, d).wait_send()
-                for d in range(1, circ_count):
-                    two_copy(h, d).wait_send()
+                arrived(M.at[par, pl.ds(*CHUNKS[h])], two_recv.at[par, h])
+            update_plane(mort_a, range(N), from_ahead, from_behind, M.at[par])
+            to_self = False
+            for way in range(2):
+                if lower + way in work_sides[way]:
+                    to_self = jnp.logical_or(
+                        to_self, jnp.logical_and(is_worker[way], own_way == way)
+                    )
+            wait_sent(A.at[mort_a], one_send, jnp.asarray(to_self))
+
+        for way in range(2):
+            @pl.when(is_worker[way])
+            def _():
+                slot = way if slots > 1 else 0
+                wait_sent(O.at[slot], two_send.at[slot], side == lower + 1 - way)
 
         @pl.when(jnp.logical_not(at_interface))
         def _():
-            update_plane(mort_a, from_ahead, from_behind, None)
+            update_plane(mort_a, range(N), from_ahead, from_behind, None)
 
         end_copy(0, behind).wait_send()
         end_copy(1, ahead).wait_send()
         return 0
 
-    def early_store():
-        others = pl.ds(1 - odd, N - 1)
-        return pltpu.make_async_copy(U.at[others], out_ref.at[0, others], store_sem.at[0])
-
     lax.fori_loop(0, STEPS, one_step, 0)
-    late = pltpu.make_async_copy(U.at[mort_a], out_ref.at[0, mort_a], store_sem.at[1])
-    late.start()
-    early_store().wait()
-    late.wait()
+
+
+def placed_work(circ_count, lower):
+    return circ_count // 4, circ_count // 2, ((lower, lower + 2), (lower, lower + 2))
 
 
 def fused(mesh, field, coeffs, reaction, step_scale, rotation):
     circ_count = mesh.shape["circ"]
     lower = mesh.shape["side"] // 2 - 1
+    first, workers, work_sides = placed_work(circ_count, lower)
+    kinds = len(set(work_sides[0]) & set(work_sides[1])) > 0
+    slots = 2 if kinds else 1
+    rows_each = circ_count // (workers * len(work_sides[0]))
     node_shape = field.shape[1:]
     face_shape = node_shape[1:]
     tile = face_shape[2:]
@@ -601,38 +697,40 @@
     anywhere = pl.BlockSpec(memory_space=pl.ANY)
     dma = pltpu.SemaphoreType.DMA
     f32 = jnp.float32
+    operands = (
+        rotation, jnp.asarray(tables), jnp.asarray(on_left), field, coeffs, reaction, step_scale
+    )
     return pl.pallas_call(
-        partial(step_kernel, lower, circ_count),
+        partial(step_kernel, lower, circ_count, first, workers, work_sides),
         out_shape=jax.ShapeDtypeStruct(field.shape, f32),
         in_specs=[smem, smem, smem] + [anywhere] * 4,
-        out_specs=anywhere,
+        out_specs=pl.BlockSpec(memory_space=pltpu.VMEM),
         scratch_shapes=[
-            pltpu.VMEM(node_shape, f32),
             pltpu.VMEM(coeffs.shape[1:], f32),
             pltpu.VMEM(node_shape, f32),
             pltpu.VMEM(node_shape, f32),
             pltpu.VMEM((N + 1,) + face_shape, f32),
-            pltpu.VMEM((2,) + face_shape, f32),
-            pltpu.VMEM(face_shape, f32),
+            pltpu.VMEM((2, slots, rows_each) + face_shape, f32),
+            pltpu.VMEM((slots, rows_each) + face_shape, f32),
             pltpu.VMEM((2,) + face_shape, f32),
             pltpu.VMEM((2,) + face_shape, f32),
             pltpu.VMEM((2,) + face_shape, f32),
             pltpu.VMEM((2,) + tile, f32),
             pltpu.VMEM((2, 2) + tile, f32),
-            dma((6,)),
-            dma((2,)),
+            dma((9,)),
             dma(()),
             dma((2,)),
             dma((2,)),
             dma((2, 2)),
-            dma((len(CHUNKS), circ_count)),
-            dma((2, len(CHUNKS), circ_count)),
-            dma((len(CHUNKS), circ_count)),
-            dma((2, len(CHUNKS), circ_count)),
             dma(()),
+            dma((2, len(CHUNKS), slots)),
+            dma((slots,)),
+            dma((2, len(CHUNKS))),
         ],
-        compiler_params=pltpu.CompilerParams(collective_id=0, has_side_effects=True),
-    )(rotation, jnp.asarray(tables), jnp.asarray(on_left), field, coeffs, reaction, step_scale)
+        compiler_params=pltpu.CompilerParams(
+            collective_id=0, has_side_effects=True, vmem_limit_bytes=24 * 2**20
+        ),
+    )(*[pltpu.with_memory_space_constraint(operand, pltpu.HBM) for operand in operands])
 
 
 def solution(mesh):

time: 53.7 us -> 44.1 us (0.82)
  Pallas kernels: 51 us -> 42.8 us
  local copies, waits for them, and re-layouts: 2.53 us -> 1.09 us
    pallas_call x1, Pallas kernels: 51 us -> 42.8 us  [fused(): pl.pallas_call(partial(step_kernel, lower, circ_count, first, workers, wo...]
    unnamed x1, local copies, waits for them, and re-layouts: 2.53 us -> 1.09 us
where the time goes in v2:
time: 44.1 us; the launch traced here: 43.9 us
  Pallas kernels  42.8 us (97%)
  local copies, waits for them, and re-layouts  1.09 us (2%)
    pallas_call x1, Pallas kernels, fused(): pl.pallas_call(partial(step_kernel, lower, circ_count, first, workers, wo...  42.8 us
    unnamed x1, local copies, waits for them, and re-layouts  1.09 us

profile of v2, /device:TPU:1, one launch (start us, length us, event | category | flops | bytes accessed | tf_op | source)
XLA Modules:
  0.0 43.9 jit_solution(16138434871141135273)
XLA Ops:
  0.0 42.8 %shard_map.73 = f32[1,7,7,7,8,128]{5,4,3,2,1,0:T(8,128)S(1)} custom-call(s32[4]{0:T(128)} %rot_ref.1, f32[147]{0:T(256)} %constant.4.clone.table_ref, s32[21]{0:T(128)} %constant.5.clone.left_ref, f32[1,7,7,7,8,128]{5,4,3,2,1,0:T(8,128)} %field_ref.1, f32[1,3,7,7,7,8,128]{6,5,4,3,2,1,0:T(8,128)} %coeffs_ref.1, f32[1,7,7,7,8,128]{5,4,3,2,1,0:T(8,128)} %reaction_ref.1, ...), custom_call_target="tpu_custom_call" | custom-call | tf_op jit(solution)/shard_map/pallas_call | solution.py:703
  42.8 1.1 %copy.9 = f32[1,7,7,7,8,128]{5,4,3,2,1,0:T(8,128)} copy(f32[1,7,7,7,8,128]{5,4,3,2,1,0:T(8,128)S(1)} %shard_map.73) | data formatting | bytes 2809856

commit v3 on v2

--- a/solution.py
+++ b/solution.py
@@ -180,6 +180,8 @@
 CHUNKS = ((0, 3), (3, 4))
 RIMS = (0, 6)
 INNER = (1, 2, 3, 4, 5)
+ONE_FIRST = (3, 2, 1, 0)
+ONE_LAST = (7, 6, 5, 4)
 FAR_FIRST = (5, 4, 7, 6, 3, 2, 1, 0)
 
 
@@ -313,31 +315,37 @@
         barrier, inc=1, device_id={"circ": circ, "side": mate}, device_id_type=MESH
     )
 
-    def greet(other_circ, other_side, when):
-        same = jnp.logical_and(circ == other_circ, side == other_side)
-
-        @pl.when(jnp.logical_and(when, jnp.logical_not(same)))
+    def greet(other_circ, other_side):
+        pl.semaphore_signal(
+            barrier, inc=1, device_id={"circ": other_circ, "side": other_side},
+            device_id_type=MESH,
+        )
+
+    def greet_other(other_circ, other_side):
+        @pl.when(jnp.logical_not(jnp.logical_and(circ == other_circ, side == other_side)))
         def _():
-            pl.semaphore_signal(
-                barrier, inc=1, device_id={"circ": other_circ, "side": other_side},
-                device_id_type=MESH,
-            )
-
-    greeted = 3
-    for other in (ahead, behind):
-        pl.semaphore_signal(
-            barrier, inc=1, device_id={"circ": other, "side": side}, device_id_type=MESH
-        )
-    for way, sides in enumerate(work_sides):
-        meets_self = jnp.logical_and(at_interface, is_worker[way]).astype(jnp.int32)
-        for work_side in sides:
+            greet(other_circ, other_side)
+
+    every_side = sorted(set(work_sides[0] + work_sides[1]))
+    works = jnp.logical_or(is_worker[0], is_worker[1])
+    meets_self = jnp.logical_and(at_interface, works).astype(jnp.int32)
+
+    @pl.when(at_interface)
+    def _():
+        for work_side in every_side:
             for w in range(first, first + workers):
-                greet(w, work_side, at_interface)
+                greet_other(w, work_side)
+
+    @pl.when(works)
+    def _():
         for c in range(circ_count):
             for face_side in (lower, lower + 1):
-                greet(c, face_side, is_worker[way])
-        greeted = greeted + jnp.where(at_interface, workers * len(sides), 0) - meets_self
-        greeted = greeted + jnp.where(is_worker[way], 2 * circ_count, 0) - meets_self
+                greet_other(c, face_side)
+
+    for other in (ahead, behind):
+        greet(other, side)
+    greeted = 3 + jnp.where(at_interface, workers * len(every_side), 0)
+    greeted = greeted + jnp.where(works, 2 * circ_count, 0) - 2 * meets_self
 
     def barrier_wait():
         pl.semaphore_wait(barrier, greeted)
@@ -397,20 +405,12 @@
                 B[0, r, c] = total
 
     def first_lines():
-        for load in later_loads[:2]:
+        for load in later_loads:
             load.wait()
 
         @pl.loop(0, N - 1)
         def _(q):
-            radial_lines(q + 1 - odd, range(N))
-
-        later_loads[2].wait()
-
-        @pl.loop(0, N - 1)
-        def _(q):
-            circ_lines(q + 1 - odd)
-
-        later_loads[3].wait()
+            radial_lines(q + 1 - odd, INNER)
 
     for load in face_loads:
         load.wait()
@@ -509,14 +509,20 @@
         def start_one(h, d):
             rows_of = pl.ds(*CHUNKS[h])
             place = paired(near, d % workers, workers)
-            group = d // workers
-            at = group % len(work_sides[0])
+            turn = d // workers
+            count = len(work_sides[0])
+            near_at = own_way if count > 1 else 0
+            at = lax.rem(near_at + turn, count)
+            to_side = jnp.where(side == lower, work_sides[0][0], work_sides[1][0])
+            for i in range(1, count):
+                other = jnp.where(side == lower, work_sides[0][i], work_sides[1][i])
+                to_side = jnp.where(at == i, other, to_side)
+            group = turn // count
             start(
-                A.at[mort_a, rows_of, :, pl.ds(group * workers + place, 1), :],
-                G.at[par, own_slot, group // len(work_sides[0]), rows_of, :, pl.ds(circ, 1), :],
-                one_send, one_recv.at[par, h, own_slot], first + place,
-                jnp.where(side == lower, work_sides[0][at], work_sides[1][at]),
-                d % workers == 0 and any(lower + w == work_sides[w][at] for w in range(2)),
+                A.at[mort_a, rows_of, :, pl.ds((group * count + at) * workers + place, 1), :],
+                G.at[par, own_slot, group, rows_of, :, pl.ds(circ, 1), :],
+                one_send, one_recv.at[par, h, own_slot], first + place, to_side,
+                d % workers == 0 and turn % count == 0,
             )
 
         def start_two(way, h, j, d):
@@ -539,12 +545,21 @@
 
             @pl.when(at_interface)
             def _():
-                for d in reversed(range(circ_count)):
+                for d in ONE_FIRST:
                     start_one(h, d)
+                if h == len(CHUNKS) - 1:
+                    for g in range(len(CHUNKS)):
+                        for d in ONE_LAST:
+                            start_one(g, d)
 
         @pl.when(t == 0)
         def _():
             first_lines()
+
+        @pl.loop(0, N - 1)
+        def _(q):
+            radial_lines(q + 1 - odd, RIMS)
+            circ_lines(q + 1 - odd)
 
         def axial_lines(columns):
             @pl.loop(0, N)
@@ -575,14 +590,6 @@
         @pl.loop(1, N - 1)
         def _(a):
             inner_plane(a, None)
-
-        conf_copy().wait_recv()
-        conf_copy().wait_send()
-        inner_plane(conf_a, C.at[par])
-
-        @pl.when(t < STEPS - 1)
-        def _():
-            partial_axial(INNER)
 
         offset = rot_ref[t]
         k = lax.div(offset, SUBSTEPS)
@@ -614,16 +621,33 @@
                         total = total + factors[m] * own[m]
                     O[slot, j, r, n] = total
 
-        for h, (begin, count) in enumerate(CHUNKS):
-            for way, project in enumerate((stator_rows, rotor_rows)):
-                @pl.when(is_worker[way])
-                def _():
-                    slot = way if slots > 1 else 0
-                    arrived(G.at[par, slot, :, pl.ds(begin, count)], one_recv.at[par, h, slot])
-                    for j in range(locals_count):
-                        project(slot, [(j, r) for r in range(begin, begin + count)])
-                        for d in FAR_FIRST:
-                            start_two(way, h, j, d)
+        def serve(way, h):
+            begin, count = CHUNKS[h]
+            slot = way if slots > 1 else 0
+            arrived(G.at[par, slot, :, pl.ds(begin, count)], one_recv.at[par, h, slot])
+            for j in range(locals_count):
+                project = (stator_rows, rotor_rows)[way]
+                project(slot, [(j, r) for r in range(begin, begin + count)])
+                for d in FAR_FIRST:
+                    start_two(way, h, j, d)
+
+        for work_side in sorted(set(work_sides[0] + work_sides[1])):
+            near_way = 0 if work_side <= lower else 1
+
+            @pl.when(jnp.logical_and(central, side == work_side))
+            def _():
+                for other, h in ((0, 0), (0, 1), (1, 0), (1, 1)):
+                    way = (near_way + other) % 2
+                    if work_side in work_sides[way]:
+                        serve(way, h)
+
+        conf_copy().wait_recv()
+        conf_copy().wait_send()
+        inner_plane(conf_a, C.at[par])
+
+        @pl.when(t < STEPS - 1)
+        def _():
+            partial_axial(INNER)
 
         end_copy(0, behind).wait_recv()
         end_copy(1, ahead).wait_recv()
@@ -632,11 +656,6 @@
 
         def rim_plane(a, extra):
             update_plane(a, RIMS, from_ahead, from_behind, extra)
-
-            @pl.when(t < STEPS - 1)
-            def _():
-                radial_lines(a, RIMS)
-                circ_lines(a)
 
         @pl.loop(1, N - 1)
         def _(a):

time: 44.1 us -> 42.7 us (0.968)
  Pallas kernels: 42.8 us -> 41.5 us
    pallas_call x1, Pallas kernels: 42.8 us -> 41.5 us  [fused(): pl.pallas_call(partial(step_kernel, lower, circ_count, first, workers, wo...]
where the time goes in v3:
time: 42.7 us; the launch traced here: 42.6 us
  Pallas kernels  41.5 us (97%)
  local copies, waits for them, and re-layouts  1.09 us (3%)
    pallas_call x1, Pallas kernels, fused(): pl.pallas_call(partial(step_kernel, lower, circ_count, first, workers, wo...  41.5 us
    unnamed x1, local copies, waits for them, and re-layouts  1.09 us

profile of v3, /device:TPU:1, one launch (start us, length us, event | category | flops | bytes accessed | tf_op | source)
XLA Modules:
  0.0 42.6 jit_solution(10399929369765200895)
XLA Ops:
  0.0 41.5 %shard_map.73 = f32[1,7,7,7,8,128]{5,4,3,2,1,0:T(8,128)S(1)} custom-call(s32[4]{0:T(128)} %rot_ref.1, f32[147]{0:T(256)} %constant.4.clone.table_ref, s32[21]{0:T(128)} %constant.5.clone.left_ref, f32[1,7,7,7,8,128]{5,4,3,2,1,0:T(8,128)} %field_ref.1, f32[1,3,7,7,7,8,128]{6,5,4,3,2,1,0:T(8,128)} %coeffs_ref.1, f32[1,7,7,7,8,128]{5,4,3,2,1,0:T(8,128)} %reaction_ref.1, ...), custom_call_target="tpu_custom_call" | custom-call | tf_op jit(solution)/shard_map/pallas_call | solution.py:722
  41.5 1.1 %copy.9 = f32[1,7,7,7,8,128]{5,4,3,2,1,0:T(8,128)} copy(f32[1,7,7,7,8,128]{5,4,3,2,1,0:T(8,128)S(1)} %shard_map.73) | data formatting | bytes 2809856
